TPU v7x, 256 devices: a 4x2x16 block of a 4x16x16 slice. The times are simulated.
256 devices in a mesh: rep: 2 (over y), ep: 64 (over z, x), tp: 2 (over core).
Axes of the slice: x: 4, y: 2, z: 16, core: 2. Of those that a mesh axis runs over, the one named last changes fastest.
The devices are a block of a 4x16x16 slice.
Arguments:
- resid: bfloat16 [8192, 1440], P(('rep', 'ep')), parts along dimension 0, may hold values from -6 to 6
- query: bfloat16 [8192, 2048], P(('rep', 'ep'), 'tp'), parts along dimension 0, may hold values from -400 to 400
- key_value_pages: bfloat16 [2, 98304, 16, 256], P(None, ('rep', 'ep'), None, 'tp'), parts along dimension 1, may hold values from -4 to 4
- page_table: int32 [8192, 12], P(('rep', 'ep')), parts along dimension 0, may hold values from 0 to 767, as said below
- ctx_len: int32 [8192], P(('rep', 'ep')), parts along dimension 0, may hold values from 2 to 192, as said below
- experts_chosen: int32 [8192, 4], P(('rep', 'ep')), parts along dimension 0, may hold values from 0 to 63, as said below
- router_logits: float32 [8192, 4], P(('rep', 'ep')), parts along dimension 0, may hold values from -25 to 300
- norm_gain: float32 [1440], replicated, may hold values from 0.25 to 1.75
- out_proj: bfloat16 [2048, 1440], P('tp'), may hold values from -0.125 to 0.125
- w_gate: bfloat16 [64, 1440, 1440], P('ep', None, 'tp'), may hold values from -0.15625 to 0.15625
- w_up: bfloat16 [64, 1440, 1440], P('ep', None, 'tp'), may hold values from -0.15625 to 0.15625
- w_down: bfloat16 [64, 1440, 1440], P('ep', 'tp'), may hold values from -3 to 3
Outputs:
- mixed: bfloat16 [8192, 1440], P(('rep', 'ep'), 'tp'), parts along dimension 0
There are 2 independent parts, one for each index of `rep`. A program takes and returns all parts, laid end to end along the dimension named above; an argument that names none is the same for every part. Nothing has to cross between parts.
Inputs may be any that keep to these rules, and one draw needn't show every extreme that they name: Each block of 64 tokens holds its own pool: the rows of page_table of one block together name each of its 768 pages once. `ctx_len`: every block of 64 tokens has a token with 192 positions. `experts_chosen`: each row names 4 different experts. Within the rows of one device no expert is named by more than 8 rows, and one expert is named by exactly 8 of them.
All inputs are finite; a program needn't handle non-finite values.
Results may differ from a plain program's by a relative error of at most 0.008.
Values may be sent and summed in bfloat16 or wider, within the bound.
A program may use at most 128 MiB of HBM per device.

v0:
```python
import math

import jax
import jax.numpy as jnp
from jax import lax
from jax.sharding import PartitionSpec as P

HEAD_WIDTH = 64


def split_up(x, dim, devices):
    lengths = x.shape
    blocks = x.reshape(*lengths[:dim], devices, lengths[dim] // devices, *lengths[dim + 1 :])
    return jnp.moveaxis(blocks, dim, 0)


def summed_on_arrival(x, axis, dim):
    devices = lax.axis_size(axis)
    blocks = lax.all_to_all(split_up(x, dim, devices), axis, 0, 0, tiled=True)
    return jnp.sum(blocks, axis=0)


def over_pieces(x, axis):
    blocks = lax.all_gather(x, axis)
    return blocks.sum(axis=0)


def copy_for_each(x, axis):
    copies = jnp.broadcast_to(x, (lax.axis_size(axis), *x.shape))
    return lax.all_to_all(copies, axis, split_axis=0, concat_axis=0, tiled=True)


def laid_out(blocks, dim):
    blocks = jnp.moveaxis(blocks, 0, dim)
    lengths = blocks.shape
    return blocks.reshape(*lengths[:dim], lengths[dim] * lengths[dim + 1], *lengths[dim + 2 :])


def gather_directly(x, axis, dim):
    blocks = copy_for_each(x, axis)
    return laid_out(blocks, dim)


def body(
    resid,
    query,
    key_value_pages,
    page_table,
    ctx_len,
    experts_chosen,
    router_logits,
    norm_gain,
    out_proj,
    w_gate,
    w_up,
    w_down,
):
    tok_rows = query.shape[0]
    model_width = resid.shape[1]
    query_heads = query.shape[1] // HEAD_WIDTH
    cache_heads = key_value_pages.shape[3] // HEAD_WIDTH
    group_width = query_heads // cache_heads
    positions = page_table.shape[1] * key_value_pages.shape[2]
    cached_keys = key_value_pages[0][page_table].reshape(
        tok_rows, positions, cache_heads, HEAD_WIDTH
    )
    cached_values = key_value_pages[1][page_table].reshape(
        tok_rows, positions, cache_heads, HEAD_WIDTH
    )
    query_block = query.reshape(tok_rows, cache_heads, group_width, HEAD_WIDTH)
    scores = jnp.einsum(
        "tgqd,tpgd->tgqp", query_block, cached_keys, preferred_element_type=jnp.float32
    ) * (1.0 / math.sqrt(HEAD_WIDTH))
    visible = jnp.arange(positions, dtype=jnp.int32)[None, :] < ctx_len[:, None]
    scores = jnp.where(visible[:, None, None, :], scores, -jnp.inf)
    row_max = jnp.max(scores, axis=3, keepdims=True)
    weights = jnp.exp(scores - row_max)
    probability = (weights / jnp.sum(weights, axis=3, keepdims=True)).astype(jnp.bfloat16)
    attended = jnp.einsum(
        "tgqp,tpgd->tgqd", probability, cached_values, preferred_element_type=jnp.float32
    )
    attended = attended.astype(jnp.bfloat16).reshape(tok_rows, query_heads * HEAD_WIDTH)
    head_part = jnp.dot(attended, out_proj, preferred_element_type=jnp.float32)
    half_cols = model_width // lax.axis_size("tp")
    offset = lax.axis_index("tp") * half_cols
    share = summed_on_arrival(head_part, "tp", 1)
    stream = lax.dynamic_slice_in_dim(resid, offset, half_cols, 1).astype(jnp.float32) + share
    mean_square = over_pieces(jnp.sum(stream * stream, axis=1), "tp") / model_width
    gain_cols = lax.dynamic_slice_in_dim(norm_gain, offset, half_cols, 0)
    normed = (stream * lax.rsqrt(mean_square + 1e-05)[:, None] * gain_cols).astype(jnp.bfloat16)
    gate_weights = jax.nn.softmax(router_logits, axis=1)
    top_count = experts_chosen.shape[1]
    local_experts = w_gate.shape[0]
    owners = lax.axis_size("ep")
    experts = local_experts * owners
    capacity = max(2, min(tok_rows, 2 * tok_rows * top_count // experts))
    chosen_flat = experts_chosen.reshape(-1)
    onehot = (chosen_flat[:, None] == jnp.arange(experts, dtype=jnp.int32)[None, :]).astype(
        jnp.int32
    )
    before = jnp.cumsum(onehot, axis=0, dtype=jnp.int32) - onehot
    slot_rank = jnp.sum(before * onehot, axis=1, dtype=jnp.int32)
    slot_index = (chosen_flat * capacity + slot_rank).reshape(tok_rows, top_count)
    slot_range = jnp.arange(experts * capacity, dtype=jnp.int32)
    placed = slot_index[:, :, None] == slot_range[None, None, :]
    dispatch = jnp.sum(placed.astype(jnp.float32), axis=1).astype(jnp.bfloat16)
    outgoing = lax.dot_general(
        dispatch, normed, (((0,), (0,)), ((), ())), preferred_element_type=jnp.float32
    )
    outgoing = outgoing.astype(jnp.bfloat16).reshape(
        owners, local_experts, capacity, normed.shape[1]
    )
    arrived_full = gather_directly(
        lax.all_to_all(outgoing, "ep", split_axis=0, concat_axis=0, tiled=True), "tp", 3
    )
    gate_value = jnp.einsum(
        "sekd,edf->sekf", arrived_full, w_gate, preferred_element_type=jnp.float32
    )
    up_value = jnp.einsum("sekd,edf->sekf", arrived_full, w_up, preferred_element_type=jnp.float32)
    hidden = (gate_value * jax.nn.sigmoid(1.702 * gate_value) * (up_value + 1.0)).astype(
        jnp.bfloat16
    )
    partial_value = jnp.einsum("sekf,efd->sekd", hidden, w_down, preferred_element_type=jnp.float32)
    finished = summed_on_arrival(partial_value, "tp", 3).astype(jnp.bfloat16)
    returned = lax.all_to_all(finished, "ep", split_axis=0, concat_axis=0, tiled=True)
    combine = jnp.sum(placed.astype(jnp.float32) * gate_weights[:, :, None], axis=1)
    expert_mix = jnp.dot(
        combine,
        returned.reshape(experts * capacity, -1).astype(jnp.float32),
        precision=lax.Precision.HIGHEST,
    )
    mixed = stream + expert_mix
    return mixed.astype(jnp.bfloat16)


def solution(mesh):
    return jax.shard_map(
        body,
        mesh=mesh,
        in_specs=(
            P(("rep", "ep"), None),
            P(("rep", "ep"), "tp"),
            P(None, ("rep", "ep"), None, "tp"),
            P(("rep", "ep"), None),
            P(("rep", "ep")),
            P(("rep", "ep"), None),
            P(("rep", "ep"), None),
            P(),
            P("tp", None),
            P("ep", None, "tp"),
            P("ep", None, "tp"),
            P("ep", "tp", None),
        ),
        out_specs=P(("rep", "ep"), "tp"),
        check_vma=False,
    )
```

profile of v0, /device:TPU:40, one launch (start us, length us, event | category | flops | bytes accessed | tf_op | source)
XLA Modules:
  0.0 228.2 jit_solution(16553985636424257385)
XLA Ops:
  0.0 0.0 copy-start
  0.0 0.0 copy-start.7
  0.0 6.7 %slice_bitcast_fusion.1 = (bf16[768,16,128]{2,1,0:T(8,128)(2,1)}, bf16[768,16,128]{2,1,0:T(8,128)(2,1)}) fusion(bf16[2,768,16,128]{3,2,1,0:T(8,128)(2,1)} %param.14), kind=kLoop, calls=%fused_computation.10 | loop fusion | bytes 12582912 | tf_op jit(solution)/shard_map/squeeze | solution.py:64
  6.7 0.0 copy-done.7
  6.7 0.1 copy.54
  6.8 0.1 reshape.125
  6.9 4.9 %gather_fusion = bf16[768,16,128]{2,1,0:T(8,128)(2,1)} fusion(bf16[768,16,128]{2,1,0:T(8,128)(2,1)} %get-tuple-element.7, s32[1024]{0:T(1024)S(1)} %pad_clamp_fusion), kind=kCustom, calls=%fused_computation | custom fusion | bytes 6294528 | tf_op jit(solution)/shard_map/gather | solution.py:64
  11.8 0.0 copy-start.4
  11.8 11.7 %reshape.110 = bf16[64,192,2,64]{3,2,1,0:T(2,128)(2,1)} reshape(bf16[768,16,128]{2,1,0:T(8,128)(2,1)} %gather_fusion) | data formatting | bytes 6291456 | tf_op jit(solution)/shard_map/reshape | solution.py:64
  23.5 0.0 copy-done.4
  23.5 0.2 reshape.111
  23.7 0.0 copy-done.9
  23.7 0.1 iota_compare_fusion.3
  23.8 4.9 %gather_fusion.1 = bf16[768,16,128]{2,1,0:T(8,128)(2,1)} fusion(bf16[768,16,128]{2,1,0:T(8,128)(2,1)} %get-tuple-element.8, s32[1024]{0:T(1024)S(1)} %pad_clamp_fusion), kind=kCustom, calls=%fused_computation.1 | custom fusion | bytes 6294528 | tf_op jit(solution)/shard_map/gather | solution.py:67
  28.7 11.6 %reshape.112 = bf16[64,192,2,64]{3,2,1,0:T(2,128)(2,1)} reshape(bf16[768,16,128]{2,1,0:T(8,128)(2,1)} %gather_fusion.1) | data formatting | bytes 6291456 | tf_op jit(solution)/shard_map/reshape | solution.py:67
  40.3 7.3 %fusion.54 = (f32[64,2,8]{2,1,0:T(2,128)S(1)}, f32[64,2,8,192]{3,2,1,0:T(8,128)}) fusion(bf16[64,2,8,64]{3,2,1,0:T(8,128)(2,1)S(1)} %reshape.111, bf16[64,192,2,64]{3,2,1,0:T(2,128)(2,1)} %reshape.110, pred[64,192]{1,0:T(8,128)(4,1)S(1)} %iota_compare_fusion.3), kind=kOutput, calls=%fused_computation.71 | convolution fusion | flops 25952448 | bytes 4079616 | tf_op jit(solution)/shard_map/sub | solution.py:77
  47.6 4.9 %fusion.31 = bf16[64,2,8,64]{3,2,1,0:T(8,128)(2,1)S(1)} fusion(bf16[64,192,2,64]{3,2,1,0:T(2,128)(2,1)} %reshape.112, f32[64,2,8,192]{3,2,1,0:T(8,128)} %get-tuple-element.10, f32[64,2,8]{2,1,0:T(2,128)S(1)} %get-tuple-element.9), kind=kOutput, calls=%fused_computation.31 | convolution fusion | flops 25624576 | bytes 4067328 | tf_op jit(solution)/shard_map/tgqp,tpgd->tgqd/dot_general | solution.py:79
  52.5 0.2 reshape.151
  52.7 0.0 copy-done
  52.7 0.0 copy-start.6
  52.7 0.0 copy-start.10
  52.7 0.0 copy-start.3
  52.8 0.0 copy-start.8
  52.8 0.0 copy-start.5
  52.8 1.7 convolution_bitcast_fusion.1
  54.5 3.7 %all-to-all-start = ((f32[2,64,720]{2,1,0:T(8,128)}), f32[2,64,720]{2,1,0:T(8,128)S(1)}, u32[]{:S(2)}, u32[]{:S(2)}) async-start(f32[2,64,720]{2,1,0:T(8,128)} %convolution_bitcast_fusion.1), calls=%async_computation | async-start | bytes 786432 | tf_op jit(solution)/shard_map/all_to_all | solution.py:19
  58.2 0.0 copy-done.6
  58.2 0.1 copy.57
  58.3 0.1 eq.42
  58.4 0.1 eq.38
  58.5 0.0 copy-done.10
  58.5 0.6 dynamic-slice
  59.8 0.0 all-to-all-done
  59.8 0.0 copy-done.3
  59.8 0.2 multiply_reduce_fusion
  60.0 0.2 dynamic-update-slice
  60.3 2.5 %all-reduce = f32[128]{0:T(128)S(1)} all-reduce(f32[128]{0:T(128)S(1)} %dynamic-update-slice), channel_id=2, replica_groups=mesh['rep'=2,'ep'=64,'tp'=2] {'tp'}, use_global_device_ids=true, to_apply=%add | all-reduce | flops 128 | bytes 1024
  62.7 0.1 reshape.139
  62.9 0.0 copy-done.8
  62.9 0.1 dynamic_slice.7
  63.0 0.6 reduce-window.6
  63.6 0.2 slice_reduce_fusion
  63.8 0.1 fusion.46
  63.9 0.1 reduce_sum.86
  64.0 0.1 copy.60
  64.1 0.0 copy-done.5
  64.2 0.2 convert_reduce_fusion
  64.3 0.5 convolution_convert_fusion
  64.8 0.3 copy.61
  65.1 71.9 %all_to_all.28 = bf16[64,1,8,720]{3,2,1,0:T(8,128)(2,1)S(1)} all-to-all(bf16[64,1,8,720]{3,2,1,0:T(8,128)(2,1)S(1)} %bitcast.128), channel_id=1, replica_groups=mesh['rep'=2,'ep'=64,'tp'=2] {'ep'}, dimensions={0} | all-to-all | bytes 1474560 | tf_op jit(solution)/shard_map/all_to_all | solution.py:114
  137.0 0.1 broadcast_in_dim.19
  137.1 5.0 %all_to_all.29 = bf16[2,64,1,8,720]{4,3,1,2,0:T(8,128)(2,1)S(1)} all-to-all(bf16[2,64,1,8,720]{4,3,1,2,0:T(8,128)(2,1)S(1)} %broadcast_in_dim.19), channel_id=1, replica_groups=mesh['rep'=2,'ep'=64,'tp'=2] {'tp'}, dimensions={0} | all-to-all | bytes 2949120 | tf_op jit(solution)/shard_map/all_to_all | solution.py:30
  142.1 1.6 copy.63
  143.7 2.1 reshape.116
  145.8 4.7 %fusion.8 = f32[64,8,720]{2,1,0:T(8,128)} fusion(bf16[64,8,1440]{2,1,0:T(8,128)(2,1)} %reshape.116, bf16[1,1440,720]{2,1,0:T(8,128)(2,1)} %param.21), kind=kOutput, calls=%fused_computation.14 | convolution fusion | flops 1061683200 | bytes 5022720 | tf_op jit(solution)/shard_map/sekd,edf->sekf/dot_general | solution.py:116
  150.6 0.0 copy-done.2
  150.6 7.6 %convolution_bitcast_fusion = f32[64,1,8,1440]{3,2,0,1:T(8,128)} fusion(bf16[1,720,1440]{2,1,0:T(8,128)(2,1)} %param.23, bf16[64,8,1440]{2,1,0:T(8,128)(2,1)S(1)} %copy-done.2, bf16[1,1440,720]{2,1,0:T(8,128)(2,1)} %param.22, f32[64,8,720]{2,1,0:T(8,128)} %fusion.8), kind=kOutput, calls=%fused_computation.7 | convolution fusion | flops 2126315520 | bytes 10045440 | tf_op jit(solution)/shard_map/sekf,efd->sekd/dot_general | solution.py:123
  158.2 5.8 %reshape.121 = f32[64,1,8,2,720]{4,3,2,0,1:T(2,128)} reshape(f32[64,1,8,1440]{3,2,0,1:T(8,128)} %convolution_bitcast_fusion) | data formatting | bytes 5898240 | tf_op jit(solution)/shard_map/reshape | solution.py:13
  164.0 2.1 copy.82
  166.1 7.2 %all_to_all.30 = f32[2,64,1,8,720]{4,3,1,2,0:T(8,128)} all-to-all(f32[2,64,1,8,720]{4,3,1,2,0:T(8,128)S(1)} %bitcast.126), channel_id=1, replica_groups=mesh['rep'=2,'ep'=64,'tp'=2] {'tp'}, dimensions={0} | all-to-all | bytes 5898240 | tf_op jit(solution)/shard_map/all_to_all | solution.py:19
  173.4 3.4 %reduce_sum.92 = bf16[64,8,720]{2,1,0:T(8,128)(2,1)} reduce(f32[2,64,1,8,720]{4,3,1,2,0:T(8,128)} %all_to_all.30, f32[]{:T(128)} %constant.9.clone.1), dimensions={0,2}, to_apply=%region_12.13 | reduce | flops 368640 | bytes 3686404 | tf_op jit(solution)/shard_map/reduce_sum | solution.py:20
  176.8 50.3 %all_to_all.31 = bf16[64,1,8,720]{3,2,1,0:T(8,128)(2,1)S(1)} all-to-all(bf16[64,1,8,720]{3,2,1,0:T(8,128)(2,1)} %bitcast.129), channel_id=1, replica_groups=mesh['rep'=2,'ep'=64,'tp'=2] {'ep'}, dimensions={0} | all-to-all | bytes 1474560 | tf_op jit(solution)/shard_map/all_to_all | solution.py:125
  227.1 1.2 fusion.34
  228.2 0.0 copy-done.1
  (16 shorter events, 0.2 us)
Async XLA Ops:
  0.0 52.7 %copy-start = (bf16[1024,1440]{0,1:T(8,128)(2,1)S(1)}, bf16[1024,1440]{0,1:T(8,128)(2,1)}, u32[]{:S(2)}) copy-start(bf16[1024,1440]{0,1:T(8,128)(2,1)} %param.20) | copy-start | bytes 8847364
  0.0 6.7 %copy-start.7 = (s32[64,12]{0,1:T(8,128)S(1)}, s32[64,12]{0,1:T(8,128)}, u32[]{:S(2)}) copy-start(s32[64,12]{0,1:T(8,128)} %param.15) | copy-start | bytes 9220
  11.8 11.7 %copy-start.4 = (bf16[64,1024]{1,0:T(8,128)(2,1)S(1)}, bf16[64,1024]{1,0:T(8,128)(2,1)}, u32[]{:S(2)}) copy-start(bf16[64,1024]{1,0:T(8,128)(2,1)} %param.13) | copy-start | bytes 393220
  11.8 11.8 %copy-start.9 = (s32[64]{0:T(128)S(1)}, s32[64]{0:T(128)}, u32[]{:S(2)}) copy-start(s32[64]{0:T(128)} %param.16) | copy-start | bytes 772
  52.7 5.5 %copy-start.6 = (s32[64,4]{0,1:T(4,128)S(1)}, s32[64,4]{0,1:T(4,128)}, u32[]{:S(2)}) copy-start(s32[64,4]{0,1:T(4,128)} %param.17) | copy-start | bytes 3076
  52.7 5.8 %copy-start.10 = (u32[256]{0:T(256)S(1)}, u32[256]{0:T(256)}, u32[]{:S(2)}) copy-start(u32[256]{0:T(256)} %constant.47) | copy-start | bytes 3076
  52.7 7.1 %copy-start.3 = (bf16[64,1440]{1,0:T(8,128)(2,1)S(1)}, bf16[64,1440]{1,0:T(8,128)(2,1)}, u32[]{:S(2)}) copy-start(bf16[64,1440]{1,0:T(8,128)(2,1)} %param.12) | copy-start | bytes 552964
  52.8 10.1 %copy-start.8 = (f32[1440]{0:T(1024)S(1)}, f32[1440]{0:T(1024)}, u32[]{:S(2)}) copy-start(f32[1440]{0:T(1024)} %param.19) | copy-start | bytes 17284
  52.8 11.3 %copy-start.5 = (f32[64,4]{0,1:T(4,128)S(1)}, f32[64,4]{0,1:T(4,128)}, u32[]{:S(2)}) copy-start(f32[64,4]{0,1:T(4,128)} %param.18) | copy-start | bytes 3076
  54.5 5.3 %all-to-all-start = ((f32[2,64,720]{2,1,0:T(8,128)}), f32[2,64,720]{2,1,0:T(8,128)S(1)}, u32[]{:S(2)}, u32[]{:S(2)}) async-start(f32[2,64,720]{2,1,0:T(8,128)} %convolution_bitcast_fusion.1), calls=%async_computation | async-start | bytes 786432 | tf_op jit(solution)/shard_map/all_to_all | solution.py:19
  145.8 4.7 %copy-start.2 = (bf16[64,8,1440]{2,1,0:T(8,128)(2,1)S(1)}, bf16[64,8,1440]{2,1,0:T(8,128)(2,1)}, u32[]{:S(2)}) copy-start(bf16[64,8,1440]{2,1,0:T(8,128)(2,1)} %reshape.116) | copy-start | bytes 4423684
  173.4 54.9 %copy-start.1 = (bf16[1024,1440]{0,1:T(8,128)(2,1)S(1)}, bf16[1024,1440]{0,1:T(8,128)(2,1)}, u32[]{:S(2)}) copy-start(bf16[1024,1440]{0,1:T(8,128)(2,1)} %param.20) | copy-start | bytes 8847364
where the time goes:
time: 229 us; the launch traced here: 228 us
  blocking collectives  137 us (60%)
  local copies, waits for them, and re-layouts  54.1 us (24%)
  matrix products  27.9 us (12%)
  other arithmetic  4.73 us (2%)
  starting transfers between devices  3.67 us (2%)
    all_to_all x1, blocking collectives, body(): lax.all_to_all(outgoing, 'ep', split_axis=0, concat_axis=0, tiled=True)  71.9 us
    all_to_all x1, blocking collectives, body(): lax.all_to_all(finished, 'ep', split_axis=0, concat_axis=0, tiled=True)  50.3 us
    reshape x1, local copies, waits for them, and re-layouts, body(): key_value_pages[0][page_table]  11.7 us
    reshape x1, local copies, waits for them, and re-layouts, body(): key_value_pages[1][page_table]  11.6 us
    reshape x2, local copies, waits for them, and re-layouts, split_up(): x.reshape(*lengths[:dim], devices, lengths[dim] // devices, *lengths[dim...  7.97 us
    dot_general x1, matrix products, body(): jnp.einsum('sekf,efd->sekd', hidden, w_down, preferred_element_type=jnp.f...  7.57 us
    sub x1, matrix products, body(): weights = jnp.exp(scores - row_max)  7.32 us
    all_to_all x1, blocking collectives, summed_on_arrival(): blocks = lax.all_to_all(split_up(x, dim, devices), axis, 0, 0, tiled=True)  7.24 us
  transfers between devices with their start and end apart: 1, of which 0 were waited for; matrix products, arithmetic and copies ran while one was open for 0% of the time, Pallas kernels for 0%

commit v1 on v0

v1 whole, which is shorter than its diff:
```python
import functools
import math

import jax
import jax.numpy as jnp
from jax import lax
from jax.experimental import pallas as pl
from jax.experimental.pallas import tpu as pltpu
from jax.sharding import PartitionSpec as P

F32, BF16 = jnp.float32, jnp.bfloat16
MESH = pl.DeviceIdType.MESH
HEAD_WIDTH = 64
LANES = 128
UNROLL = 8
ALONG_X = 4
CHUNKS = 4


def up_to(n, m):
    return -(-n // m) * m


def attend_kernel(pt_ref, len_ref, q_ref, kv_ref, o_ref, kv, s_ref, p_ref, sem):
    tokens, rows, lanes = q_ref.shape
    pages = pt_ref.shape[1]
    page = kv_ref.shape[2]
    positions = pages * page
    half = rows // 2
    copies = [pltpu.make_async_copy(kv_ref.at[i], kv.at[i], sem.at[i]) for i in range(2)]
    for copy in copies:
        copy.start()
    copies[0].wait()

    def scores(g, carry):
        for i in range(UNROLL):
            t = g * UNROLL + i
            keys = jnp.concatenate([kv[0, pt_ref[t, j]] for j in range(pages)], axis=0)
            s = lax.dot_general(q_ref[t], keys, (((1,), (1,)), ((), ())), preferred_element_type=F32)
            pos = lax.broadcasted_iota(jnp.int32, (rows, positions), 1)
            s_ref[t] = jnp.where(pos < len_ref[t], s * (1.0 / math.sqrt(HEAD_WIDTH)), -1e30)
        return carry

    lax.fori_loop(0, tokens // UNROLL, scores, 0)

    def soften(g, carry):
        s = s_ref[pl.ds(g * UNROLL, UNROLL)]
        w = jnp.exp(s - jnp.max(s, axis=2, keepdims=True))
        p_ref[pl.ds(g * UNROLL, UNROLL)] = (w / jnp.sum(w, axis=2, keepdims=True)).astype(BF16)
        return carry

    lax.fori_loop(0, tokens // UNROLL, soften, 0)
    copies[1].wait()

    def mix(g, carry):
        for i in range(UNROLL):
            t = g * UNROLL + i
            vals = jnp.concatenate([kv[1, pt_ref[t, j]] for j in range(pages)], axis=0)
            o = jnp.dot(p_ref[t], vals, preferred_element_type=F32)
            lane = lax.broadcasted_iota(jnp.int32, (half, lanes), 1)
            o_ref[pl.ds(pl.multiple_of(t * half, half), half), :] = jnp.where(
                lane < HEAD_WIDTH, o[:half], o[half:]
            )
        return carry

    lax.fori_loop(0, tokens // UNROLL, mix, 0)


def lay_queries(query):
    tokens = query.shape[0]
    q = query.reshape(tokens, 2, -1, HEAD_WIDTH)
    zero = jnp.zeros_like(q[:, 0])
    first = jnp.concatenate([q[:, 0], zero], axis=2)
    return jnp.concatenate([first, jnp.concatenate([zero, q[:, 1]], axis=2)], axis=1)


def attend(query, kv, page_table, ctx_len):
    tokens = query.shape[0]
    laid = lay_queries(query)
    half = laid.shape[1] // 2
    positions = kv.shape[2] * page_table.shape[1]
    vmem = pl.BlockSpec(memory_space=pltpu.VMEM)
    smem = pl.BlockSpec(memory_space=pltpu.SMEM)
    return pl.pallas_call(
        attend_kernel,
        out_shape=jax.ShapeDtypeStruct((tokens * half, 2 * HEAD_WIDTH), F32),
        in_specs=[smem, smem, vmem, pl.BlockSpec(memory_space=pl.ANY)],
        out_specs=vmem,
        scratch_shapes=[
            pltpu.VMEM(kv.shape, BF16),
            pltpu.VMEM((tokens, 2 * half, positions), F32),
            pltpu.VMEM((tokens, 2 * half, positions), BF16),
            pltpu.SemaphoreType.DMA((2,)),
        ],
        name="attend",
    )(page_table, ctx_len, laid, kv)


def layer_kernel(
    cap,
    nz,
    att_ref,
    resid_ref,
    meta_ref,
    gain_ref,
    wo_ref,
    wg_ref,
    wu_ref,
    wd_ref,
    out_ref,
    wo,
    wg,
    wu,
    wd,
    part_s,
    part_r,
    nrm,
    strm,
    agb,
    mb,
    sel,
    xin,
    pin,
    gate_s,
    hid_s,
    ybuf,
    yrec,
    ysend,
    yin,
    ct,
    mix,
    rss,
    rsr,
    w_sem,
    ps_sem,
    pr_sem,
    ag_s,
    ag_r,
    mt_s,
    mt_r,
    x_s,
    x_r,
    p_s,
    p_r,
    y_s,
    y_r,
    b_s,
    b_r,
    rs_s,
    rs_r,
):
    nx = ALONG_X
    far = nz // 2
    tokens, width = resid_ref.shape
    half = out_ref.shape[1]
    wide = agb.shape[3]
    rows = tokens // CHUNKS
    slots = 2 * cap
    e = lax.axis_index("ep")
    t = lax.axis_index("tp")
    z, x = e // nx, lax.rem(e, nx)

    def at(zz, xx, tt):
        return {"ep": zz * nx + xx, "tp": tt}

    right = at(lax.rem(z + 1, nz), x, t)
    left = at(lax.rem(z + nz - 1, nz), x, t)
    ahead = (right, left)
    partner = at(z, x, 1 - t)
    plus = [None] + [at(z, lax.rem(x + j, nx), t) for j in range(1, nx)]
    minus = [None] + [at(z, lax.rem(x + nx - j, nx), t) for j in range(1, nx)]

    barrier = pltpu.get_barrier_semaphore()
    for d in (right, left, partner, *plus[1:]):
        pl.semaphore_signal(barrier, inc=1, device_id=d, device_id_type=MESH)

    def remote(src, dst, ss, rs, dev):
        return pltpu.make_async_remote_copy(
            src_ref=src, dst_ref=dst, send_sem=ss, recv_sem=rs, device_id=dev, device_id_type=MESH
        )

    pairs = wo_ref.shape[0] // (2 * HEAD_WIDTH)
    loads = []
    for p in range(pairs):
        for g in range(2):
            loads.append(
                pltpu.make_async_copy(
                    wo_ref.at[pl.ds((g * pairs + p) * HEAD_WIDTH, HEAD_WIDTH)],
                    wo.at[pl.ds((2 * p + g) * HEAD_WIDTH, HEAD_WIDTH)],
                    w_sem.at[2 * p + g],
                )
            )
    n = 2 * pairs
    w_loads = [
        pltpu.make_async_copy(wg_ref, wg.at[pl.ds(0, width)], w_sem.at[n]),
        pltpu.make_async_copy(wu_ref, wu.at[pl.ds(0, width)], w_sem.at[n + 1]),
        pltpu.make_async_copy(wd_ref, wd, w_sem.at[n + 2]),
    ]
    for c in loads + w_loads:
        c.start()
    pad = wg.shape[0] - width
    wg[pl.ds(width, pad), :] = jnp.zeros((pad, wg.shape[1]), BF16)
    wu[pl.ds(width, pad), :] = jnp.zeros((pad, wu.shape[1]), BF16)

    acc = None
    for q in range(0, pairs, 2):
        for c in loads[2 * q : 2 * q + 4]:
            c.wait()
        a = jnp.concatenate(
            [att_ref[pl.ds(p, tokens, stride=pairs), :].astype(BF16) for p in (q, q + 1)], axis=1
        )
        term = jnp.dot(a, wo[pl.ds(q * LANES, 2 * LANES), :], preferred_element_type=F32)
        part_s[:, :width] = term if q == 0 else part_s[:, :width] + term
    fill = part_s.shape[1] - width
    part_s[:, width:] = jnp.zeros((tokens, fill), F32)

    pl.semaphore_wait(barrier, 2 + nx)
    swap = remote(part_s, part_r, ps_sem, pr_sem, partner)
    swap.start()

    mb[0, 0] = meta_ref[0]
    mb[far, 1] = meta_ref[1]
    lane = lax.broadcasted_iota(jnp.int32, (2 * cap, LANES), 1)
    sub = lax.broadcasted_iota(jnp.int32, (2 * cap, LANES), 0)
    r_i = lax.broadcasted_iota(jnp.int32, (LANES, LANES), 0)
    c_i = lax.broadcasted_iota(jnp.int32, (LANES, LANES), 1)
    same = (r_i < tokens) == (c_i < tokens)
    earlier = jnp.where((r_i < c_i) & same, 1.0, 0.0).astype(BF16)

    def ag_copy(s, d, c):
        src = agb.at[far, 1, pl.ds(c * rows, rows)] if s == 1 else agb.at[s - 1, d, pl.ds(c * rows, rows)]
        dst = agb.at[far, 0, pl.ds(c * rows, rows)] if s == far else agb.at[s, d, pl.ds(c * rows, rows)]
        return remote(src, dst, ag_s.at[s, d, c], ag_r.at[s, d, c], ahead[d])

    def mt_copy(s, d):
        src = (mb.at[0, 0] if d == 0 else mb.at[far, 1]) if s == 1 else mb.at[s - 1, d]
        return remote(src, mb.at[s, d], mt_s.at[s, d], mt_r.at[s, d], ahead[d])

    def travels(s, d, c):
        return s < far or (c < CHUNKS // 2) == (d == 0)

    def meta_travels(s, d):
        return s < far or d == 0

    sent = []

    def go(copy):
        copy.start()
        sent.append(copy)

    for d in range(2):
        go(mt_copy(1, d))
    swap.wait_recv()
    for c in range(CHUNKS):
        at_rows = pl.ds(c * rows, rows)
        total = part_s[at_rows, :] + part_r[at_rows, :]
        stream = total[:, :width] + resid_ref[at_rows, :].astype(F32)
        ms = jnp.sum(stream * stream, axis=1, keepdims=True) / width
        normed = (stream * lax.rsqrt(ms + 1e-05) * gain_ref[...]).astype(BF16)
        nrm[0, at_rows, :] = normed[:, :wide]
        nrm[1, at_rows, : width - wide] = normed[:, wide:]
        nrm[1, at_rows, width - wide :] = jnp.zeros((rows, 2 * wide - width), BF16)
        strm[at_rows, :width] = stream
        agb[far, 1, at_rows, :] = nrm[t, at_rows, :]
        for d in range(2):
            go(ag_copy(1, d, c))
    swap.wait_send()

    def halves(ref, at_rows):
        v = ref[at_rows, :]
        return v[:, :wide], pltpu.roll(v, v.shape[1] - half, 1)[:, :wide]

    def select(g):
        m = jnp.where(lane[:8] < tokens, mb[g, 0], mb[g, 1])
        chosen, gates = m[:4], m[4:]
        named, weight = [], []
        for j in range(nx):
            own = (z * nx + lax.rem(x + j, nx)).astype(F32)
            hit = chosen == own
            named.append(jnp.sum(jnp.where(hit, 1.0, 0.0), axis=0, keepdims=True))
            weight.append(jnp.sum(jnp.where(hit, gates, 0.0), axis=0, keepdims=True))
        a = jnp.concatenate(named + named, axis=0)
        rank = jnp.dot(a.astype(BF16), earlier, preferred_element_type=F32)
        blocks = []
        for j in range(nx):
            right_slot = rank[j : j + 1] == lax.rem(sub, cap).astype(F32)
            right_side = (sub < cap) == (lane < tokens)
            block = jnp.where(right_slot & right_side & (named[j] > 0.5), 1.0, 0.0)
            blocks.append(block)
            ct[g - 1, pl.ds(j * slots, slots), :] = block * weight[j]
        place = jnp.concatenate(blocks, axis=0).astype(BF16)
        rows_in = jnp.concatenate([agb[g, 0], agb[g, 1]], axis=0)
        picked = jnp.dot(place, rows_in, preferred_element_type=F32).astype(BF16)
        xin[g, 0] = picked[:slots]
        for j in range(1, nx):
            sel[g, j] = picked[j * slots : (j + 1) * slots]
            go(remote(sel.at[g, j], xin.at[g, j], x_s.at[g, j], x_r.at[g, j], plus[j]))

    def pass_on(g):
        for j in range(1, nx):
            remote(sel.at[g, j], xin.at[g, j], x_s.at[g, j], x_r.at[g, j], plus[j]).wait_recv()
        go(remote(xin.at[g], pin.at[g], p_s.at[g], p_r.at[g], partner))

    def both(g, w):
        lhs0 = xin[g].reshape(nx * slots, wide)
        lhs1 = pin[g].reshape(nx * slots, wide)
        own = pl.ds(pl.multiple_of(t * wide, wide), wide)
        other = pl.ds(pl.multiple_of((1 - t) * wide, wide), wide)
        return jnp.dot(lhs0, w[own, :], preferred_element_type=F32) + jnp.dot(
            lhs1, w[other, :], preferred_element_type=F32
        )

    def gate_up_a(g):
        if g == 1:
            for c in w_loads:
                c.wait()
        remote(xin.at[g], pin.at[g], p_s.at[g], p_r.at[g], partner).wait_recv()
        gate_s[...] = both(g, wg)

    def gate_up_b(g):
        up = both(g, wu)
        gate = gate_s[...]
        hid_s[...] = (gate * jax.nn.sigmoid(1.702 * gate) * (up + 1.0)).astype(BF16)

    def down_a(g):
        ybuf[g, 0] = jnp.dot(hid_s[...], wd[:, :wide], preferred_element_type=F32)

    def down_b(g):
        m = nx * slots
        hi = jnp.dot(hid_s[...], wd[:, wide:], preferred_element_type=F32)
        for r in range(0, m, 16):
            lo = ybuf[g, 0, pl.ds(r, 16), :]
            v = jnp.concatenate([lo, hi[r : r + 16], jnp.zeros((16, 2 * wide - width), F32)], axis=1)
            ybuf[g, 1, pl.ds(r, 16), :] = pltpu.roll(v, 2 * wide - half, 1)[:, :wide]
        go(remote(ybuf.at[g, 1 - t], yrec.at[g], y_s.at[g], y_r.at[g], partner))

    def send_back(g):
        remote(ybuf.at[g, 1 - t], yrec.at[g], y_s.at[g], y_r.at[g], partner).wait_recv()
        y = (ybuf[g, t] + yrec[g]).astype(BF16)
        yin[g, 0] = y[:slots]
        for j in range(1, nx):
            ysend[g, j] = y[j * slots : (j + 1) * slots]
            go(remote(ysend.at[g, j], yin.at[g, j], b_s.at[g, j], b_r.at[g, j], minus[j]))

    def combine(g):
        for j in range(1, nx):
            remote(ysend.at[g, j], yin.at[g, j], b_s.at[g, j], b_r.at[g, j], minus[j]).wait_recv()
        c = ct[g - 1].T
        hi = c.astype(BF16)
        lo = (c - hi.astype(F32)).astype(BF16)
        y = yin[g].reshape(nx * slots, wide)
        mix[g - 1] = jnp.dot(hi, y, preferred_element_type=F32) + jnp.dot(lo, y, preferred_element_type=F32)

    plan = {
        0: ((pass_on, 2), (down_a, 3), (send_back, 4)),
        1: ((down_b, 3),),
        2: ((gate_up_a, 2), (combine, 5)),
        3: ((gate_up_b, 2), (select, 0)),
    }
    for s in range(1, 2 * far + 1):
        if s <= far:
            for d in range(2):
                if meta_travels(s, d):
                    mt_copy(s, d).wait_recv()
                    if s < far and meta_travels(s + 1, d):
                        go(mt_copy(s + 1, d))
        for c in range(CHUNKS):
            if s <= far:
                for d in range(2):
                    cc = c if d == 0 or s < far else CHUNKS - 1 - c
                    if travels(s, d, cc):
                        ag_copy(s, d, cc).wait_recv()
                        if s < far and travels(s + 1, d, cc):
                            go(ag_copy(s + 1, d, cc))
            for stage, lag in plan[c]:
                if 1 <= s - lag <= far:
                    stage(s - lag)

    def rs_copy(k, d, c):
        return remote(
            rss.at[k, d, pl.ds(c * rows, rows)],
            rsr.at[k - 1, d, pl.ds(c * rows, rows)],
            rs_s.at[k, d, c],
            rs_r.at[k, d, c],
            ahead[1 - d],
        )

    def give(k, d, c):
        at_rows = pl.ds(c * rows, rows)
        own_rows = pl.ds((0 if k == far else d * tokens) + c * rows, rows)
        v = mix[k - 1, own_rows, :]
        if k < far and travels(k + 1, d, c):
            rs_copy(k + 1, d, c).wait_recv()
            v = v + rsr[k, d, at_rows, :].astype(F32)
        rss[k, d, at_rows, :] = v.astype(BF16)
        go(rs_copy(k, d, c))

    for k in range(far, 0, -1):
        for c in range(CHUNKS):
            for d in range(2):
                cc = c if d else (c + CHUNKS // 2) % CHUNKS
                if travels(k, d, cc):
                    give(k, d, cc)
    for c in range(CHUNKS):
        cc = (c + CHUNKS // 2) % CHUNKS
        at_rows = pl.ds(cc * rows, rows)
        lo, hi = halves(strm, at_rows)
        stream = jnp.where(t == 0, lo, hi)
        v = stream + mix[far - 1, pl.ds(tokens + cc * rows, rows), :]
        for d in range(2):
            rs_copy(1, d, cc).wait_recv()
            v = v + rsr[0, d, at_rows, :].astype(F32)
        out_ref[at_rows, :] = v[:, :half].astype(BF16)
    for copy in sent:
        copy.wait_send()


def rest(att, resid, meta, gain, out_proj, w_gate, w_up, w_down, cap, nz):
    tokens, width = resid.shape
    half = width // 2
    wide = up_to(half, LANES)
    far = nz // 2
    slots = 2 * cap
    hidden = w_gate.shape[1]
    vmem = pl.BlockSpec(memory_space=pltpu.VMEM)
    hbm = pl.BlockSpec(memory_space=pl.ANY)
    V, S = pltpu.VMEM, pltpu.SemaphoreType.DMA
    g1 = far + 1
    scratch = [
        V(out_proj.shape, BF16),
        V((2 * wide, hidden), BF16),
        V((2 * wide, hidden), BF16),
        V(w_down.shape, BF16),
        V((tokens, 2 * wide), F32),
        V((tokens, 2 * wide), F32),
        V((2, tokens, wide), BF16),
        V((tokens, 2 * wide), F32),
        V((g1, 2, tokens, wide), BF16),
        V((g1, 2, 8, LANES), F32),
        V((g1, ALONG_X, slots, wide), BF16),
        V((g1, ALONG_X, slots, wide), BF16),
        V((g1, ALONG_X, slots, wide), BF16),
        V((ALONG_X * slots, hidden), F32),
        V((ALONG_X * slots, hidden), BF16),
        V((g1, 2, ALONG_X * slots, wide), F32),
        V((g1, ALONG_X * slots, wide), F32),
        V((g1, ALONG_X, slots, wide), BF16),
        V((g1, ALONG_X, slots, wide), BF16),
        V((far, ALONG_X * slots, LANES), F32),
        V((far, 2 * tokens, wide), F32),
        V((g1, 2, tokens, wide), BF16),
        V((g1, 2, tokens, wide), BF16),
        S((2 * (out_proj.shape[0] // (2 * HEAD_WIDTH)) + 3,)),
        S,
        S,
        S((g1, 2, CHUNKS)),
        S((g1, 2, CHUNKS)),
        S((g1, 2)),
        S((g1, 2)),
        S((g1, ALONG_X)),
        S((g1, ALONG_X)),
        S((g1,)),
        S((g1,)),
        S((g1,)),
        S((g1,)),
        S((g1, ALONG_X)),
        S((g1, ALONG_X)),
        S((g1, 2, CHUNKS)),
        S((g1, 2, CHUNKS)),
    ]
    return pl.pallas_call(
        functools.partial(layer_kernel, cap, nz),
        out_shape=jax.ShapeDtypeStruct((tokens, half), BF16),
        in_specs=[vmem] * 4 + [hbm] * 4,
        out_specs=vmem,
        scratch_shapes=scratch,
        compiler_params=pltpu.CompilerParams(collective_id=0, has_side_effects=True, vmem_limit_bytes=56 << 20),
        name="layer",
    )(att, resid, meta, gain, out_proj, w_gate, w_up, w_down)


def body(
    resid,
    query,
    key_value_pages,
    page_table,
    ctx_len,
    experts_chosen,
    router_logits,
    norm_gain,
    out_proj,
    w_gate,
    w_up,
    w_down,
):
    tokens, top = experts_chosen.shape
    owners = lax.axis_size("ep")
    experts = w_gate.shape[0] * owners
    cap = max(2, min(tokens, 2 * tokens * top // experts))
    att = attend(query, key_value_pages, page_table, ctx_len)
    gates = jax.nn.softmax(router_logits, axis=1)
    empty = jnp.full((top, LANES - tokens), -1.0, F32)
    chosen_t = experts_chosen.T.astype(F32)
    none = jnp.zeros((top, LANES - tokens), F32)
    meta = jnp.stack(
        [
            jnp.concatenate([jnp.concatenate([chosen_t, empty], 1), jnp.concatenate([gates.T, none], 1)], 0),
            jnp.concatenate([jnp.concatenate([empty, chosen_t], 1), jnp.concatenate([none, gates.T], 1)], 0),
        ]
    )
    return rest(
        att, resid, meta, norm_gain[None], out_proj, w_gate[0], w_up[0], w_down[0], cap, owners // ALONG_X
    )


def solution(mesh):
    return jax.shard_map(
        body,
        mesh=mesh,
        in_specs=(
            P(("rep", "ep"), None),
            P(("rep", "ep"), "tp"),
            P(None, ("rep", "ep"), None, "tp"),
            P(("rep", "ep"), None),
            P(("rep", "ep")),
            P(("rep", "ep"), None),
            P(("rep", "ep"), None),
            P(),
            P("tp", None),
            P("ep", None, "tp"),
            P("ep", None, "tp"),
            P("ep", "tp", None),
        ),
        out_specs=P(("rep", "ep"), "tp"),
        check_vma=False,
    )
```

time: 229 us -> 126 us (0.55)
  blocking collectives: 137 us -> 0 us
  Pallas kernels: 0 us -> 113 us
  local copies, waits for them, and re-layouts: 54.1 us -> 8.32 us
  matrix products: 27.9 us -> 0 us
  starting transfers between devices: 3.67 us -> 0 us
    all_to_all x4 -> x0, blocking collectives: 134 us -> none  [the longest x1 71.9 us: body(): lax.all_to_all(outgoing, 'ep', split_axis=0, concat_axis=0, tiled=True)]
    pallas_call x0 -> x2, Pallas kernels: none -> 113 us  [the longest x1 103 us: rest(): pl.pallas_call(functools.partial(layer_kernel, cap, nz), out_shape=jax.Sh...]
    reshape x6 -> x1, local copies, waits for them, and re-layouts: 31.6 us -> 1.12 us  [lay_queries(): q = query.reshape(tokens, 2, -1, HEAD_WIDTH)]
    dot_general x6 -> x0, matrix products: 20.6 us -> none  [the longest x1 7.57 us: body(): jnp.einsum('sekf,efd->sekd', hidden, w_down, preferred_element_type=jnp.f...]
    gather x2 -> x0, local copies, waits for them, and re-layouts: 9.76 us -> none  [the longest x1 4.9 us: body(): key_value_pages[1][page_table]]
    sub x1 -> x0, matrix products: 7.32 us -> none  [body(): weights = jnp.exp(scores - row_max)]
    squeeze x1, local copies, waits for them, and re-layouts: 6.72 us -> 0.02 us  [lay_queries(): first = jnp.concatenate([q[:, 0], zero], axis=2)]
    unnamed x26 -> x5, local copies, waits for them, and re-layouts: 0.98 us -> 5.89 us
  transfers between devices with their start and end apart: 1 -> 0, of which waited for: 0 -> 0; matrix products, arithmetic and copies ran while one was open for 0% -> 0% of each run, Pallas kernels for 0% -> 0%
where the time goes in v1:
time: 126 us; the launch traced here: 125 us
  Pallas kernels  113 us (90%)
  local copies, waits for them, and re-layouts  8.32 us (7%)
  other arithmetic  4.26 us (3%)
    pallas_call x1, Pallas kernels, rest(): pl.pallas_call(functools.partial(layer_kernel, cap, nz), out_shape=jax.Sh...  103 us
    pallas_call x1, Pallas kernels, attend(): pl.pallas_call(attend_kernel, out_shape=jax.ShapeDtypeStruct((tokens * ha...  9.81 us
    unnamed x5, local copies, waits for them, and re-layouts  5.89 us

profile of v1, /device:TPU:40, one launch (start us, length us, event | category | flops | bytes accessed | tf_op | source)
XLA Modules:
  0.0 125.3 jit_solution(14312247284066564792)
XLA Ops:
  0.0 0.7 reduce_max.9
  0.7 0.7 fusion.5
  1.4 0.7 divide_bitcast_fusion
  2.1 0.7 convert_bitcast_fusion
  2.8 0.1 fusion.4
  2.9 0.6 pad_maximum_fusion.meta_ref
  3.5 1.3 %broadcast_in_dim.2.gain_ref = f32[1,1440]{1,0:T(1,128)} reshape(f32[1440]{0:T(1024)} %param.19) | data formatting | bytes 11520 | tf_op jit(solution)/shard_map/broadcast_in_dim | solution.py:512
  4.8 1.4 %copy.17.pt_ref = s32[64,12]{1,0:T(8,128)} copy(s32[64,12]{0,1:T(8,128)} %param.15) | data formatting | bytes 6144 | tf_op args[3]
  6.1 1.1 reshape.5
  7.3 0.8 fusion.2.q_ref
  8.1 0.0 copy-start
  8.1 9.8 %attend.1.att_ref = f32[512,128]{1,0:T(8,128)} custom-call(s32[64,12]{1,0:T(8,128)} %copy.17.pt_ref, s32[64]{0:T(128)} %len_ref.1, bf16[64,16,128]{2,1,0:T(8,128)(2,1)} %fusion.2.q_ref, bf16[2,768,16,128]{3,2,1,0:T(8,128)(2,1)} %kv_ref.1), custom_call_target="tpu_custom_call" | custom-call | tf_op jit(solution)/shard_map/attend/pallas_call | solution.py:84
  17.9 0.0 copy-done
  17.9 2.9 %copy.18.wo_ref = bf16[1024,1440]{1,0:T(8,128)(2,1)} copy(bf16[1024,1440]{0,1:T(8,128)(2,1)S(1)} %copy-done) | data formatting | bytes 5898240 | tf_op args[8]
  20.9 102.9 %layer.1 = bf16[64,720]{1,0:T(8,128)(2,1)} custom-call(f32[512,128]{1,0:T(8,128)} %attend.1.att_ref, bf16[64,1440]{1,0:T(8,128)(2,1)} %resid_ref.1, f32[2,8,128]{2,1,0:T(8,128)} %pad_maximum_fusion.meta_ref, f32[1,1440]{1,0:T(1,128)} %broadcast_in_dim.2.gain_ref, bf16[1024,1440]{1,0:T(8,128)(2,1)} %copy.18.wo_ref, bf16[1440,720]{1,0:T(8,128)(2,1)} %bitcast.19, ...), custom_call_target="tpu_custom_call" | custom-call | tf_op jit(solution)/shard_map/layer/pallas_call | solution.py:471
  123.8 1.5 %copy.22 = bf16[64,720]{1,0:T(8,128)(2,1)} copy(bf16[64,720]{1,0:T(8,128)(2,1)} %layer.1) | data formatting | bytes 184320
  (1 shorter events, 0.0 us)
Async XLA Ops:
  8.1 9.8 %copy-start = (bf16[1024,1440]{0,1:T(8,128)(2,1)S(1)}, bf16[1024,1440]{0,1:T(8,128)(2,1)}, u32[]{:S(2)}) copy-start(bf16[1024,1440]{0,1:T(8,128)(2,1)} %param.20) | copy-start | bytes 8847364
